TPU v7x, 32 devices: a whole 2x2x4 slice. The times are simulated.
32 devices in a mesh: group: 8 (over y, x, core), shard: 4 (over z).
Axes of the slice: x: 2, y: 2, z: 4, core: 2. Of those that a mesh axis runs over, the one named last changes fastest.
Arguments:
- momentum: bfloat16 [8, 7168, 2048], P(None, ('group', 'shard'))
- gradient: bfloat16 [8, 7168, 2048], P(None, ('group', 'shard'))
- q_prev: bfloat16 [8, 3, 2048, 128], P('group', None, 'shard'), may hold values from -6 to 6
- owner_group: int32 [8], replicated, may hold values from 0 to 7, as said below
- group_counts: int32 [8], replicated, may hold values from 0 to 3, as said below
Outputs:
- momentum_next: bfloat16 [8, 7168, 2048], P(None, ('group', 'shard'))
- update: bfloat16 [8, 7168, 2048], P(None, ('group', 'shard'))
- q_next: bfloat16 [8, 3, 2048, 128], P('group', None, 'shard')
Inputs may be any that keep to these rules, and one draw needn't show every extreme that they name: `owner_group`: each group owns at most 3 experts and some group owns exactly 3; a group's experts fill its slots 0, 1, ... in increasing expert order. `group_counts`: entry g is the number of experts whose owner_group is g, except for one or two groups that own some experts, where it is one less; it equals 3 for some group that owns 3 experts.
All inputs are finite; a program needn't handle non-finite values.
Results may differ from a plain program's by a relative error of at most 0.0059.
Values may be sent and summed in bfloat16 or wider, within the bound.
A program may use at most 128 MiB of HBM per device.

v0:
```python
import math
import jax
import jax.numpy as jnp
from jax import lax
from jax.sharding import PartitionSpec as P

D = 7168
RANK = 128
stability_offset = 1e-06
momentum_decay = 0.6
AXES = ("group", "shard")


def owner_slots(owner_group):
    experts = owner_group.shape[0]
    expert_ids = jnp.arange(experts, dtype=jnp.int32)
    same_owner = owner_group[:, None] == owner_group[None, :]
    earlier = expert_ids[None, :] < expert_ids[:, None]
    return jnp.sum((same_owner & earlier).astype(jnp.int32), axis=1)


def shards(momentum, gradient, q_prev, owner_group, group_counts):
    me = lax.axis_index("group")
    experts, block, hidden = momentum.shape
    cap, share_rows, rank = q_prev.shape[1:]
    slot_of = owner_slots(owner_group)
    keep = slot_of < group_counts[owner_group]
    mine = keep & (owner_group == me)
    pieces = jnp.zeros((experts, share_rows, rank), jnp.bfloat16)
    for j in range(cap):
        pick = mine & (slot_of == j)
        pieces = jnp.where(pick[:, None, None], q_prev[0, j][None], pieces)
    q_one = lax.psum_scatter(pieces, "group", scatter_dimension=0, tiled=True)
    q_shard = lax.all_gather(q_one, "shard", axis=1, tiled=True)
    q_full = lax.all_gather(q_shard, "group", axis=0, tiled=True)
    combined = (momentum.astype(jnp.float32) + gradient.astype(jnp.float32)).astype(jnp.bfloat16)
    left_raw = jnp.einsum("erh,ehk->erk", combined, q_full, preferred_element_type=jnp.float32)
    squares = lax.psum(jnp.sum(left_raw * left_raw, axis=1), AXES)
    left_unit = (left_raw * lax.rsqrt(squares + stability_offset)[:, None, :]).astype(jnp.bfloat16)
    part = jnp.einsum("erh,erk->ehk", combined, left_unit, preferred_element_type=jnp.float32)
    part = lax.psum_scatter(part, "group", scatter_dimension=0, tiled=True)
    share = lax.psum_scatter(part, "shard", scatter_dimension=1, tiled=True)
    right = lax.all_gather(share.astype(jnp.bfloat16), "shard", axis=1, tiled=True)
    right = lax.all_gather(right, "group", axis=0, tiled=True)
    right32 = right.astype(jnp.float32)
    scale = lax.rsqrt(jnp.mean(right32 * right32, axis=1) + stability_offset)
    q_new = (right32 * scale[:, None, :]).astype(jnp.bfloat16)
    update = (
        jnp.einsum("erk,ehk->erh", left_unit, q_new, preferred_element_type=jnp.float32)
        * math.sqrt(D / RANK)
    ).astype(jnp.bfloat16)
    low_rank = jnp.einsum("erk,ehk->erh", left_unit, right, preferred_element_type=jnp.float32)
    momentum_next = (combined.astype(jnp.float32) - (1.0 - momentum_decay) * low_rank).astype(
        jnp.bfloat16
    )
    rows = lax.dynamic_slice_in_dim(q_new, lax.axis_index("shard") * share_rows, share_rows, axis=1)
    kept = []
    for j in range(cap):
        pick = mine & (slot_of == j)
        kept.append(jnp.sum(jnp.where(pick[:, None, None], rows, jnp.zeros_like(rows)), axis=0))
    return (momentum_next, update, jnp.stack(kept)[None])


def solution(mesh):
    return jax.shard_map(
        shards,
        mesh=mesh,
        in_specs=(
            P(None, AXES, None),
            P(None, AXES, None),
            P("group", None, "shard", None),
            P(),
            P(),
        ),
        out_specs=(P(None, AXES, None), P(None, AXES, None), P("group", None, "shard", None)),
        check_vma=False,
    )
```

profile of v0, /device:TPU:0, one launch (start us, length us, event | category | flops | bytes accessed | tf_op | source)
XLA Modules:
  0.0 346.7 jit_solution(16092060516255264329)
XLA Ops:
  7.2 0.9 convert_reduce_fusion
  8.1 0.7 compare_select_fusion
  8.8 0.6 gather_fusion
  9.5 0.7 compare_and_fusion.2
  10.1 1.1 slice_bitcast_fusion.2
  11.2 1.2 select_select_fusion
  12.5 38.8 %reduce-scatter.4.cloned.1.call-done = bf16[1,512,128]{2,1,0:T(8,128)(2,1)} async-done(((bf16[8,512,128]{2,1,0:T(8,128)(2,1)}), bf16[1,512,128]{2,1,0:T(8,128)(2,1)}) %reduce-scatter.4.cloned.1.call-update) | async-done | bytes 131088 | tf_op jit(solution)/shard_map/reduce_scatter | solution.py:33
  51.3 17.1 %all_gather.12 = bf16[1,2048,128]{2,1,0:T(8,128)(2,1)} all-gather(bf16[1,512,128]{2,1,0:T(8,128)(2,1)} %reduce-scatter.4.cloned.1.call-done), channel_id=1, replica_groups=mesh['group'=8,'shard'=4] {'shard'}, dimensions={1}, use_global_device_ids=true | all-gather | bytes 655360 | tf_op jit(solution)/shard_map/all_gather | solution.py:34
  68.5 35.9 %all-gather.3.cloned.1.call-done = bf16[8,2048,128]{2,1,0:T(8,128)(2,1)} async-done(((bf16[1,2048,128]{2,1,0:T(8,128)(2,1)}), bf16[8,2048,128]{2,1,0:T(8,128)(2,1)}) %all-gather.3.cloned.1.call-update) | async-done | bytes 4194320 | tf_op jit(solution)/shard_map/all_gather | solution.py:35
  104.4 8.7 %multiply_reduce_fusion = (f32[8,128]{1,0:T(8,128)S(1)}, f32[8,224,128]{2,1,0:T(8,128)S(1)}) fusion(bf16[8,2048,128]{2,1,0:T(8,128)(2,1)} %all-gather.3.cloned.1.call-done, bf16[8,224,2048]{2,1,0:T(8,128)(2,1)} %param.6, bf16[8,224,2048]{2,1,0:T(8,128)(2,1)} %param.5), kind=kOutput, calls=%fused_computation.13 | convolution fusion | flops 954661888 | bytes 19795968 | tf_op jit(solution)/shard_map/erh,ehk->erk/dot_general | solution.py:37
  113.1 39.3 %psum.7 = f32[8,128]{1,0:T(8,128)S(1)} all-reduce(f32[8,128]{1,0:T(8,128)S(1)} %get-tuple-element.13), channel_id=1, replica_groups=mesh['group'=8,'shard'=4] {'group','shard'}, use_global_device_ids=true, to_apply=%region_3.4 | all-reduce | flops 1024 | bytes 8192 | tf_op jit(solution)/shard_map/psum | solution.py:38
  152.4 0.1 multiply_convert_fusion.1
  152.5 11.6 %fusion.3 = f32[8,2048,128]{2,1,0:T(8,128)} fusion(bf16[8,224,128]{2,1,0:T(8,128)(2,1)S(1)} %multiply_convert_fusion.1, bf16[8,224,2048]{2,1,0:T(8,128)(2,1)} %param.6, bf16[8,224,2048]{2,1,0:T(8,128)(2,1)} %param.5), kind=kOutput, calls=%fused_computation.29 | convolution fusion | flops 954204160 | bytes 23527424 | tf_op jit(solution)/shard_map/erh,erk->ehk/dot_general | solution.py:40
  164.2 72.4 %reduce-scatter.6.cloned.1.call-done = f32[1,2048,128]{2,1,0:T(8,128)} async-done(((f32[8,2048,128]{2,1,0:T(8,128)}), f32[1,2048,128]{2,1,0:T(8,128)}) %reduce-scatter.6.cloned.1.call-update) | async-done | bytes 1048592 | tf_op jit(solution)/shard_map/reduce_scatter | solution.py:41
  236.6 29.4 %reduce-scatter.8.cloned.1.call-done = f32[1,512,128]{2,1,0:T(8,128)} async-done(((f32[1,2048,128]{2,1,0:T(8,128)}), f32[1,512,128]{2,1,0:T(8,128)}) %reduce-scatter.8.cloned.1.call-update) | async-done | bytes 262160 | tf_op jit(solution)/shard_map/reduce_scatter | solution.py:42
  266.0 1.0 convert_element_type.45
  267.0 16.8 %all_gather.14 = bf16[1,2048,128]{2,1,0:T(8,128)(2,1)} all-gather(bf16[1,512,128]{2,1,0:T(8,128)(2,1)S(1)} %convert_element_type.45), channel_id=1, replica_groups=mesh['group'=8,'shard'=4] {'shard'}, dimensions={1}, use_global_device_ids=true | all-gather | bytes 655360 | tf_op jit(solution)/shard_map/all_gather | solution.py:43
  283.8 34.9 %all-gather.5.cloned.1.call-done = bf16[8,2048,128]{2,1,0:T(8,128)(2,1)} async-done(((bf16[1,2048,128]{2,1,0:T(8,128)(2,1)}), bf16[8,2048,128]{2,1,0:T(8,128)(2,1)}) %all-gather.5.cloned.1.call-update) | async-done | bytes 4194320 | tf_op jit(solution)/shard_map/all_gather | solution.py:44
  318.8 3.0 fusion
  321.8 3.1 fusion.1
  324.9 5.1 %multiply_convert_fusion = bf16[8,224,2048]{2,1,0:T(8,128)(2,1)} fusion(bf16[8,224,128]{2,1,0:T(8,128)(2,1)S(1)} %multiply_convert_fusion.1, bf16[8,2048,128]{2,1,0:T(8,128)(2,1)S(1)} %fusion.1), kind=kOutput, calls=%fused_computation.1 | convolution fusion | flops 946864128 | bytes 11993088 | tf_op jit(solution)/shard_map/erk,ehk->erh/dot_general | solution.py:49
  330.1 0.6 select_reduce_fusion.2
  330.7 0.8 maximum_bitcast_fusion
  331.5 8.7 %subtract_convert_fusion = bf16[8,224,2048]{2,1,0:T(8,128)(2,1)} fusion(bf16[8,224,128]{2,1,0:T(8,128)(2,1)S(1)} %multiply_convert_fusion.1, bf16[8,2048,128]{2,1,0:T(8,128)(2,1)S(1)} %copy-done.1, bf16[8,224,2048]{2,1,0:T(8,128)(2,1)} %param.6, bf16[8,224,2048]{2,1,0:T(8,128)(2,1)} %param.5), kind=kOutput, calls=%fused_computation.2 | convolution fusion | flops 968884224 | bytes 26673152 | tf_op jit(solution)/shard_map/erk,ehk->erh/dot_general | solution.py:52
  (18 shorter events, 0.3 us)
Async XLA Ops:
  7.2 1.6 copy-start
  7.2 44.1 %reduce-scatter.4.cloned.1.call-start = ((), (), s32[]{:S(2)}) async-start(), calls=%async_computation.3 | async-start | bytes 1179648 | tf_op jit(solution)/shard_map/reduce_scatter | solution.py:33
  12.4 91.9 %all-gather.3.cloned.1.call-start = ((), (), s32[]{:S(2)}) async-start(), calls=%async_computation.4 | async-start | bytes 4718592 | tf_op jit(solution)/shard_map/all_gather | solution.py:35
  68.4 168.1 %reduce-scatter.6.cloned.1.call-start = ((), (), s32[]{:S(2)}) async-start(), calls=%async_computation.5 | async-start | bytes 9437184 | tf_op jit(solution)/shard_map/reduce_scatter | solution.py:41
  164.1 101.9 %reduce-scatter.8.cloned.1.call-start = ((), (), s32[]{:S(2)}) async-start(), calls=%async_computation.6 | async-start | bytes 1310720 | tf_op jit(solution)/shard_map/reduce_scatter | solution.py:42
  236.6 82.2 %all-gather.5.cloned.1.call-start = ((), (), s32[]{:S(2)}) async-start(), calls=%async_computation.7 | async-start | bytes 4718592 | tf_op jit(solution)/shard_map/all_gather | solution.py:44
  324.9 6.6 %copy-start.1 = (bf16[8,2048,128]{2,1,0:T(8,128)(2,1)S(1)}, bf16[8,2048,128]{2,1,0:T(8,128)(2,1)}, u32[]{:S(2)}) copy-start(bf16[8,2048,128]{2,1,0:T(8,128)(2,1)} %all-gather.5.cloned.1.call-done) | copy-start | bytes 12582916
Sparse Core Ops, SparseCore 0:
  12.5 38.6 reduce-scatter.3
  68.5 35.7 all-gather.2
  164.3 72.2 reduce-scatter.5
  238.7 27.2 reduce-scatter.7
  283.9 34.7 all-gather.4
where the time goes:
time: 347 us
  waiting for transfers between devices  211 us (61%)
  blocking collectives  73.3 us (21%)
  matrix products  34.2 us (10%)
  between operations  13.8 us (4%)
  other arithmetic  12.1 us (3%)
    reduce_scatter x1, waiting for transfers between devices, shards(): part = lax.psum_scatter(part, 'group', scatter_dimension=0, tiled=True)  72.4 us
    psum x1, blocking collectives, shards(): squares = lax.psum(jnp.sum(left_raw * left_raw, axis=1), AXES)  39.3 us
    reduce_scatter x1, waiting for transfers between devices, shards(): q_one = lax.psum_scatter(pieces, 'group', scatter_dimension=0, tiled=True)  38.8 us
    all_gather x1, waiting for transfers between devices, shards(): q_full = lax.all_gather(q_shard, 'group', axis=0, tiled=True)  35.9 us
    all_gather x1, waiting for transfers between devices, shards(): right = lax.all_gather(right, 'group', axis=0, tiled=True)  34.9 us
    reduce_scatter x1, waiting for transfers between devices, shards(): share = lax.psum_scatter(part, 'shard', scatter_dimension=1, tiled=True)  29.4 us
    all_gather x1, blocking collectives, shards(): q_shard = lax.all_gather(q_one, 'shard', axis=1, tiled=True)  17.1 us
    all_gather x1, blocking collectives, shards(): lax.all_gather(share.astype(jnp.bfloat16), 'shard', axis=1, tiled=True)  16.8 us
  transfers between devices with their start and end apart: 5, of which 5 were waited for; matrix products, arithmetic and copies ran while one was open for 0% of the time, Pallas kernels for 0%

commit v1 on v0

--- a/solution.py
+++ b/solution.py
@@ -35,7 +35,7 @@
     q_full = lax.all_gather(q_shard, "group", axis=0, tiled=True)
     combined = (momentum.astype(jnp.float32) + gradient.astype(jnp.float32)).astype(jnp.bfloat16)
     left_raw = jnp.einsum("erh,ehk->erk", combined, q_full, preferred_element_type=jnp.float32)
-    squares = lax.psum(jnp.sum(left_raw * left_raw, axis=1), AXES)
+    squares = jnp.sum(lax.all_gather(jnp.sum(left_raw * left_raw, axis=1), AXES), axis=0)
     left_unit = (left_raw * lax.rsqrt(squares + stability_offset)[:, None, :]).astype(jnp.bfloat16)
     part = jnp.einsum("erh,erk->ehk", combined, left_unit, preferred_element_type=jnp.float32)
     part = lax.psum_scatter(part, "group", scatter_dimension=0, tiled=True)

time: 347 us -> 373 us (1.075)
  blocking collectives: 73.3 us -> 102 us
    all_gather x0 -> x1, blocking collectives: none -> 68.4 us  [shards(): lax.all_gather(jnp.sum(left_raw * left_raw, axis=1), AXES)]
    psum x1 -> x0, blocking collectives: 39.3 us -> none  [shards(): squares = lax.psum(jnp.sum(left_raw * left_raw, axis=1), AXES)]
where the time goes in v1:
time: 373 us; the launch traced here: 372 us
  waiting for transfers between devices  208 us (56%)
  blocking collectives  102 us (27%)
  matrix products  34.2 us (9%)
  between operations  13.8 us (4%)
  other arithmetic  12.1 us (3%)
    reduce_scatter x1, waiting for transfers between devices, shards(): part = lax.psum_scatter(part, 'group', scatter_dimension=0, tiled=True)  68.9 us
    all_gather x1, blocking collectives, shards(): lax.all_gather(jnp.sum(left_raw * left_raw, axis=1), AXES)  68.4 us
    reduce_scatter x1, waiting for transfers between devices, shards(): q_one = lax.psum_scatter(pieces, 'group', scatter_dimension=0, tiled=True)  38.8 us
    all_gather x1, waiting for transfers between devices, shards(): q_full = lax.all_gather(q_shard, 'group', axis=0, tiled=True)  35.9 us
    all_gather x1, waiting for transfers between devices, shards(): right = lax.all_gather(right, 'group', axis=0, tiled=True)  35 us
    reduce_scatter x1, waiting for transfers between devices, shards(): share = lax.psum_scatter(part, 'shard', scatter_dimension=1, tiled=True)  29.4 us
    all_gather x1, blocking collectives, shards(): q_shard = lax.all_gather(q_one, 'shard', axis=1, tiled=True)  17.1 us
    all_gather x1, blocking collectives, shards(): lax.all_gather(share.astype(jnp.bfloat16), 'shard', axis=1, tiled=True)  16.8 us
  transfers between devices with their start and end apart: 5, of which 5 were waited for; matrix products, arithmetic and copies ran while one was open for 0% of the time, Pallas kernels for 0%

profile of v1, /device:TPU:0, one launch (start us, length us, event | category | flops | bytes accessed | tf_op | source)
XLA Modules:
  0.0 372.3 jit_solution(12797015611868373413)
XLA Ops:
  7.2 0.9 convert_reduce_fusion
  8.1 0.7 compare_select_fusion
  8.8 0.6 gather_fusion
  9.5 0.7 compare_and_fusion.2
  10.1 1.1 slice_bitcast_fusion.2
  11.2 1.2 select_select_fusion
  12.5 38.8 %reduce-scatter.4.cloned.1.call-done = bf16[1,512,128]{2,1,0:T(8,128)(2,1)} async-done(((bf16[8,512,128]{2,1,0:T(8,128)(2,1)}), bf16[1,512,128]{2,1,0:T(8,128)(2,1)}) %reduce-scatter.4.cloned.1.call-update) | async-done | bytes 131088 | tf_op jit(solution)/shard_map/reduce_scatter | solution.py:33
  51.3 17.1 %all_gather.18 = bf16[1,2048,128]{2,1,0:T(8,128)(2,1)} all-gather(bf16[1,512,128]{2,1,0:T(8,128)(2,1)} %reduce-scatter.4.cloned.1.call-done), channel_id=1, replica_groups=mesh['group'=8,'shard'=4] {'shard'}, dimensions={1}, use_global_device_ids=true | all-gather | bytes 655360 | tf_op jit(solution)/shard_map/all_gather | solution.py:34
  68.5 35.9 %all-gather.4.cloned.1.call-done = bf16[8,2048,128]{2,1,0:T(8,128)(2,1)} async-done(((bf16[1,2048,128]{2,1,0:T(8,128)(2,1)}), bf16[8,2048,128]{2,1,0:T(8,128)(2,1)}) %all-gather.4.cloned.1.call-update) | async-done | bytes 4194320 | tf_op jit(solution)/shard_map/all_gather | solution.py:35
  104.4 8.7 %multiply_reduce_fusion = (f32[8,128]{1,0:T(8,128)S(1)}, f32[8,224,128]{2,1,0:T(8,128)S(1)}) fusion(bf16[8,2048,128]{2,1,0:T(8,128)(2,1)} %all-gather.4.cloned.1.call-done, bf16[8,224,2048]{2,1,0:T(8,128)(2,1)} %param.6, bf16[8,224,2048]{2,1,0:T(8,128)(2,1)} %param.5), kind=kOutput, calls=%fused_computation.13 | convolution fusion | flops 954661888 | bytes 19795968 | tf_op jit(solution)/shard_map/erh,ehk->erk/dot_general | solution.py:37
  113.1 68.4 %all-gather = f32[256,128]{1,0:T(8,128)S(1)} all-gather(f32[8,128]{1,0:T(8,128)S(1)} %get-tuple-element.13), channel_id=2, replica_groups=mesh['group'=8,'shard'=4] {'group','shard'}, dimensions={0}, use_global_device_ids=true | all-gather | bytes 135168 | tf_op jit(solution)/shard_map/all_gather | solution.py:38
  181.5 0.1 multiply_convert_fusion.1
  181.6 11.6 %fusion.3 = f32[8,2048,128]{2,1,0:T(8,128)} fusion(bf16[8,224,128]{2,1,0:T(8,128)(2,1)S(1)} %multiply_convert_fusion.1, bf16[8,224,2048]{2,1,0:T(8,128)(2,1)} %param.6, bf16[8,224,2048]{2,1,0:T(8,128)(2,1)} %param.5), kind=kOutput, calls=%fused_computation.30 | convolution fusion | flops 954204160 | bytes 23527424 | tf_op jit(solution)/shard_map/erh,erk->ehk/dot_general | solution.py:40
  193.3 68.9 %reduce-scatter.6.cloned.1.call-done = f32[1,2048,128]{2,1,0:T(8,128)} async-done(((f32[8,2048,128]{2,1,0:T(8,128)}), f32[1,2048,128]{2,1,0:T(8,128)}) %reduce-scatter.6.cloned.1.call-update) | async-done | bytes 1048592 | tf_op jit(solution)/shard_map/reduce_scatter | solution.py:41
  262.2 29.4 %reduce-scatter.8.cloned.1.call-done = f32[1,512,128]{2,1,0:T(8,128)} async-done(((f32[1,2048,128]{2,1,0:T(8,128)}), f32[1,512,128]{2,1,0:T(8,128)}) %reduce-scatter.8.cloned.1.call-update) | async-done | bytes 262160 | tf_op jit(solution)/shard_map/reduce_scatter | solution.py:42
  291.6 1.0 convert_element_type.45
  292.5 16.8 %all_gather.22 = bf16[1,2048,128]{2,1,0:T(8,128)(2,1)} all-gather(bf16[1,512,128]{2,1,0:T(8,128)(2,1)S(1)} %convert_element_type.45), channel_id=1, replica_groups=mesh['group'=8,'shard'=4] {'shard'}, dimensions={1}, use_global_device_ids=true | all-gather | bytes 655360 | tf_op jit(solution)/shard_map/all_gather | solution.py:43
  309.4 35.0 %all-gather.6.cloned.1.call-done = bf16[8,2048,128]{2,1,0:T(8,128)(2,1)} async-done(((bf16[1,2048,128]{2,1,0:T(8,128)(2,1)}), bf16[8,2048,128]{2,1,0:T(8,128)(2,1)}) %all-gather.6.cloned.1.call-update) | async-done | bytes 4194320 | tf_op jit(solution)/shard_map/all_gather | solution.py:44
  344.3 3.0 fusion
  347.4 3.1 fusion.1
  350.5 5.1 %multiply_convert_fusion = bf16[8,224,2048]{2,1,0:T(8,128)(2,1)} fusion(bf16[8,224,128]{2,1,0:T(8,128)(2,1)S(1)} %multiply_convert_fusion.1, bf16[8,2048,128]{2,1,0:T(8,128)(2,1)S(1)} %fusion.1), kind=kOutput, calls=%fused_computation.1 | convolution fusion | flops 946864128 | bytes 11993088 | tf_op jit(solution)/shard_map/erk,ehk->erh/dot_general | solution.py:49
  355.6 0.6 select_reduce_fusion.2
  356.3 0.8 maximum_bitcast_fusion
  357.1 8.7 %subtract_convert_fusion = bf16[8,224,2048]{2,1,0:T(8,128)(2,1)} fusion(bf16[8,224,128]{2,1,0:T(8,128)(2,1)S(1)} %multiply_convert_fusion.1, bf16[8,2048,128]{2,1,0:T(8,128)(2,1)S(1)} %copy-done.1, bf16[8,224,2048]{2,1,0:T(8,128)(2,1)} %param.6, bf16[8,224,2048]{2,1,0:T(8,128)(2,1)} %param.5), kind=kOutput, calls=%fused_computation.2 | convolution fusion | flops 968884224 | bytes 26673152 | tf_op jit(solution)/shard_map/erk,ehk->erh/dot_general | solution.py:52
  (19 shorter events, 0.4 us)
Async XLA Ops:
  7.2 1.6 copy-start
  7.2 44.1 %reduce-scatter.4.cloned.1.call-start = ((), (), s32[]{:S(2)}) async-start(), calls=%async_computation.3 | async-start | bytes 1179648 | tf_op jit(solution)/shard_map/reduce_scatter | solution.py:33
  12.4 91.9 %all-gather.4.cloned.1.call-start = ((), (), s32[]{:S(2)}) async-start(), calls=%async_computation.4 | async-start | bytes 4718592 | tf_op jit(solution)/shard_map/all_gather | solution.py:35
  68.4 193.7 %reduce-scatter.6.cloned.1.call-start = ((), (), s32[]{:S(2)}) async-start(), calls=%async_computation.5 | async-start | bytes 9437184 | tf_op jit(solution)/shard_map/reduce_scatter | solution.py:41
  193.2 98.3 %reduce-scatter.8.cloned.1.call-start = ((), (), s32[]{:S(2)}) async-start(), calls=%async_computation.6 | async-start | bytes 1310720 | tf_op jit(solution)/shard_map/reduce_scatter | solution.py:42
  262.2 82.2 %all-gather.6.cloned.1.call-start = ((), (), s32[]{:S(2)}) async-start(), calls=%async_computation.7 | async-start | bytes 4718592 | tf_op jit(solution)/shard_map/all_gather | solution.py:44
  350.5 6.6 %copy-start.1 = (bf16[8,2048,128]{2,1,0:T(8,128)(2,1)S(1)}, bf16[8,2048,128]{2,1,0:T(8,128)(2,1)}, u32[]{:S(2)}) copy-start(bf16[8,2048,128]{2,1,0:T(8,128)(2,1)} %all-gather.6.cloned.1.call-done) | copy-start | bytes 12582916
Sparse Core Ops, SparseCore 0:
  12.5 38.6 reduce-scatter.3
  68.5 35.7 all-gather.3
  193.4 68.7 reduce-scatter.5
  264.3 27.2 reduce-scatter.7
  309.5 34.7 all-gather.5
